TPU v7x, 128 devices: a whole 4x4x4 slice. The times are simulated.
128 devices in a mesh: gx: 32 (over y, x, core), gy: 4 (over z).
Axes of the slice: x: 4, y: 4, z: 4, core: 2. Of those that a mesh axis runs over, the one named last changes fastest.
Arguments:
- sources: bfloat16 [8192, 8, 128], P(('gx', 'gy')), may hold values from -6 to 6
- owners: int32 [8192, 1], P(('gx', 'gy')), may hold values from 0 to 31; in each aligned block of 64 rows (0 to 63, 64 to 127, ...) at most 4 rows name the same one
- strip_rows: int32 [8192], P(('gx', 'gy')), may hold values from 0 to 255
- panel_counts: int32 [8192], P(('gx', 'gy')), may hold values from 1 to 128
- arrival_bins: int32 [8192, 4, 128], P('gx'), may hold values from 0 to 254
- arrival_fracs: float32 [8192, 4, 128], P('gx'), may hold values from 0 to 1
- gain_table: bfloat16 [8192, 8, 4, 1024], P('gx'), may hold values from -0.125 to 0.125
Outputs:
- signals: float32 [1024, 4, 256], P(('gx', 'gy'))
Inputs may be any that keep to these rules, and one draw needn't show every extreme that they name: `owners`: among the rows of one device, at most 4 strips name one patch, a bound that some block reaches.
All inputs are finite; a program needn't handle non-finite values.
Results may differ from a plain program's by a relative error of at most 0.0044.
Values may be sent and summed in bfloat16 or wider, within the bound.
A program may use at most 768 MiB of HBM per device.

v0:
```python
import jax
import jax.numpy as jnp
from jax import lax
from jax.experimental import pallas as pl
from jax.experimental.pallas import tpu as pltpu
from jax.sharding import PartitionSpec as P

MESH = pl.DeviceIdType.MESH
F32 = jnp.float32
BF16 = jnp.bfloat16
I32 = jnp.int32

NX = 32
NZ = 4
ND = NX * NZ
STRIPS = 64
TERMS = 8
PANELS = 128
ROWS = 256
NBIN = 256
CAP = 4
TIMES = 1024
HALF = NBIN // 2
TALL = HALF + 16
UNROLL = 4
NT = (((1,), (1,)), ((), ()))


def iota(shape, dim):
    return lax.broadcasted_iota(I32, shape, dim)


def dot(a, b):
    return jnp.dot(a, b, preferred_element_type=F32)


def dot_nt(a, b):
    return lax.dot_general(a, b, NT, preferred_element_type=F32)


SIDES = (0, 1, 3, 2)
DIRECT = ()


def wait_bytes(ref, blocks, sem):
    block = ref.at[pl.ds(0, blocks)]
    pltpu.make_async_copy(block, block, sem).wait()


def kernel(
    src_hbm, own_hbm, row_hbm, cnt_hbm, bins_hbm, fracs_hbm, gains_hbm, out_ref,
    send_s, send_m, got_s, got_m, bins, fracs, gains, weights, rows, arrived,
    chosen, select, sums, row_at, send_q, got_q, send_p, got_p, in_sem, gain_sem, ss_sem, sm_sem, sp_sem, rs_sem, rm_sem, rp_sem,
    zs_sem, zr_sem, za_sem, zb_sem, ms_sem, mr_sem, qs_sem, qr_sem, ds_sem,
    src_ref, own_ref, row_ref, cnt_ref,
):
    mx = lax.axis_index("gx")
    mz = lax.axis_index("gy")
    scopes = []

    def phase(name=None):
        if scopes:
            scopes.pop().__exit__(None, None, None)
        if name:
            scopes.append(jax.named_scope(name))
            scopes[-1].__enter__()

    def gain_copy(tile):
        return pltpu.make_async_copy(gains_hbm.at[:, tile, mz // 2], gains.at[tile], gain_sem.at[tile])

    barrier = pltpu.get_barrier_semaphore()
    up, down, across = (lax.rem(mz + i, NZ) for i in (1, 3, 2))

    @pl.loop(1, NX)
    def _(step):
        peer = lax.rem(mx + step, NX)
        pl.semaphore_signal(barrier, inc=1, device_id={"gx": peer, "gy": mz}, device_id_type=MESH)

    pl.semaphore_signal(barrier, inc=1, device_id={"gx": mx, "gy": across}, device_id_type=MESH)

    if not DIRECT:
        for plane in (up, down):
            pl.semaphore_signal(barrier, inc=1, device_id={"gx": mx, "gy": plane}, device_id_type=MESH)

    @pl.loop(0, 8 * len(DIRECT))
    def _(step):
        peer = (mx // 8 * 8 + step // 8 * 8 + lax.rem(mx + step, 8)) & (NX - 1)
        for plane in (up, down):
            pl.semaphore_signal(barrier, inc=1, device_id={"gx": peer, "gy": plane}, device_id_type=MESH)

    small = [
        pltpu.make_async_copy(hbm, ref, in_sem.at[2 + i])
        for i, (hbm, ref) in enumerate(
            ((own_hbm, own_ref), (row_hbm, row_ref), (cnt_hbm, cnt_ref), (src_hbm, src_ref))
        )
    ]
    for copy in small:
        copy.start()
    bins_copy = pltpu.make_async_copy(bins_hbm, bins, in_sem.at[0])
    fracs_copy = pltpu.make_async_copy(fracs_hbm, fracs, in_sem.at[1])
    bins_copy.start()
    fracs_copy.start()

    def weigh(first, last):
        where_b = iota((TALL, PANELS), 0).astype(F32).astype(BF16)

        @pl.loop(first, last)
        def _(step):
            start = step * 8 * NZ + mz
            low = (bins[pl.ds(start, 8, stride=NZ), :] & (HALF - 1)).astype(F32)
            high = low + 1.0
            frac = fracs[pl.ds(start, 8, stride=NZ), :]
            rest = 1.0 - frac
            low, high, frac, rest = (x.astype(BF16) for x in (low, high, frac, rest))
            for i in range(8):
                pick = lambda x: jnp.broadcast_to(x[i : i + 1, :], (TALL, PANELS))
                value = jnp.where(where_b == pick(high), pick(frac), jnp.zeros((), BF16))
                value = jnp.where(where_b == pick(low), pick(rest), value)
                weights[step * 8 + i] = value

    phase("prep")
    for copy in small:
        copy.wait()
    owner = own_ref[...]
    row1 = row_ref[...] + 1
    hot = (iota((NX, STRIPS), 0) == owner).astype(F32)
    upto = (iota((STRIPS, STRIPS), 0) <= iota((STRIPS, STRIPS), 1)).astype(F32).astype(BF16)
    seen = dot(hot.astype(BF16), upto)
    place = jnp.sum(hot * (seen - 1.0), axis=0, keepdims=True)
    slot = owner.astype(F32) * CAP + place
    lane_of = (iota((128, STRIPS), 0) == (place.astype(I32) + mx * CAP)).astype(F32).astype(BF16)
    meta = dot_nt((hot * row1.astype(F32)).astype(BF16), lane_of)
    for j in range(NX):
        send_m[j] = meta[j : j + 1, :]
    wide = (iota((STRIPS, STRIPS * TERMS), 0) == iota((STRIPS, STRIPS * TERMS), 1) >> 3)
    wide = wide.astype(F32).astype(BF16)
    slot_c = dot(jnp.broadcast_to(slot, (8, STRIPS)).astype(BF16), wide)[0:1].astype(I32)
    tall = (iota((STRIPS * TERMS, STRIPS), 1) == iota((STRIPS * TERMS, STRIPS), 0) >> 3)
    tall = tall.astype(F32).astype(BF16)
    count = dot_nt(tall, jnp.broadcast_to(cnt_ref[...].astype(F32), (128, STRIPS)).astype(BF16))
    live = iota((STRIPS * TERMS, PANELS), 1).astype(F32) < count
    masked = jnp.where(live, src_ref[...].astype(F32), 0.0).astype(BF16)
    term = iota((1, STRIPS * TERMS), 1) & 7
    for kk in range(4):
        dest = jnp.where((term & 3) == kk, 2 * slot_c + (term >> 2), -1)
        placing = (iota((ND * 2, STRIPS * TERMS), 0) == dest).astype(F32).astype(BF16)
        placed = dot(placing, masked)
        send_s[:, :, kk * 128 : (kk + 1) * 128] = placed.reshape(NX, 8, 128).astype(BF16)

    phase("barrier")
    pl.semaphore_wait(barrier, NX + (16 * len(DIRECT) or 2))

    my = mx // 8

    def strip_copy(j, side):
        return pltpu.make_async_remote_copy(
            src_ref=send_s.at[j], dst_ref=got_s.at[mz * NX + mx], send_sem=ss_sem,
            recv_sem=rs_sem.at[side], device_id={"gx": j, "gy": mz}, device_id_type=MESH,
        )

    def meta_copy(j):
        return pltpu.make_async_remote_copy(
            src_ref=send_m.at[j], dst_ref=got_m.at[mx], send_sem=sm_sem, recv_sem=rm_sem,
            device_id={"gx": j, "gy": mz}, device_id_type=MESH,
        )

    def direct_copy(j, side, way):
        return pltpu.make_async_remote_copy(
            src_ref=send_s.at[j], dst_ref=got_s.at[mz * NX + mx], send_sem=ds_sem,
            recv_sem=zr_sem.at[way, side], device_id={"gx": j, "gy": (up, down)[way]},
            device_id_type=MESH,
        )

    phase("send")
    for side in SIDES:
        for i in range(8):
            j = lax.rem(my + NZ - side, 4) * 8 + lax.rem(mx + i, 8)
            if side or i:
                strip_copy(j, side).start()
    @pl.loop(1, NX)
    def _(step):
        meta_copy(lax.rem(mx + step, NX)).start()

    for side in DIRECT:
        for i in range(8):
            j = lax.rem(my + NZ - side, 4) * 8 + lax.rem(mx + i, 8)
            for way in range(2):
                direct_copy(j, side, way).start()

    for tile in range(8):
        gain_copy(tile).start()
    got_s[mz * NX + mx] = send_s[mx]
    got_m[mx] = send_m[mx]

    def group(z, side, half=None):
        first = z * NX + lax.rem(my + side, 4) * 8
        if half is None:
            return got_s.at[pl.ds(first, 8)]
        return got_s.at[pl.ds(first + half * 4, 4)]

    def ring_copy(side, way):
        block = group(mz, side)
        return pltpu.make_async_remote_copy(
            src_ref=block, dst_ref=block, send_sem=zs_sem.at[way, side],
            recv_sem=zr_sem.at[way, side], device_id={"gx": mx, "gy": (up, down)[way]},
            device_id_type=MESH,
        )

    def relay_copy(side, way):
        block = group((down, up)[way], side, way)
        return pltpu.make_async_remote_copy(
            src_ref=block, dst_ref=block, send_sem=za_sem.at[way, side],
            recv_sem=zb_sem.at[way, side], device_id={"gx": mx, "gy": (up, down)[way]},
            device_id_type=MESH,
        )

    def weigh_some(count):
        first = done[0]
        done[0] = min(first + count, ROWS // 8)
        if done[0] > first:
            phase("weights")
            weigh(first, done[0])

    def choose_some(count):
        first = done[1]
        done[1] = min(first + count, 8)
        if done[1] == first:
            return
        phase("choose")

        @pl.loop(first, done[1])
        def _(step):
            n = step // 2
            for u in range(8):
                at = lax.rem(step, 2) * 8 + u
                taken = pl.ds(pl.multiple_of(at * 256, 256), 256)
                pair = [gains.at[2 * n + i].reshape(ROWS * TERMS * 2, 128)[taken, :] for i in range(2)]
                value = dot(select[...], jnp.concatenate(pair, axis=1))
                for i in range(2):
                    half = value[:, i * 128 : (i + 1) * 128].astype(BF16)
                    chosen[2 * n + i, pl.ds(pl.multiple_of(at * 128, 128), 128), :] = half

    done = [0, 0]
    select[...] = (
        iota((128, 256), 1) == 2 * iota((128, 256), 0) + lax.rem(mz, 2)
    ).astype(F32).astype(BF16)
    bins_copy.wait()
    fracs_copy.wait()
    weigh_some(ROWS)
    for i, side in enumerate(SIDES):
        phase("near")
        wait_bytes(got_s, 8 if side else 7, rs_sem.at[side])
        for way in range(0 if side in DIRECT else 2):
            ring_copy(side, way).start()
        if i == 0:
            for tile in range(8):
                gain_copy(tile).wait()
        choose_some(1)
    phase("meta")
    wait_bytes(got_m, NX - 1, rm_sem)
    row_at[mz] = jnp.sum(got_m[...].reshape(NX, 128), axis=0, keepdims=True)

    def row_copy(i):
        peer = (up, down, across)[i]
        return pltpu.make_async_remote_copy(
            src_ref=row_at.at[mz], dst_ref=row_at.at[mz], send_sem=ms_sem.at[i],
            recv_sem=mr_sem.at[i], device_id={"gx": mx, "gy": peer}, device_id_type=MESH,
        )

    for i in range(3):
        row_copy(i).start()

    half = iota((1, 2 * ND), 1) & 1
    twice = (iota((128, 2 * 128), 0) == iota((128, 2 * 128), 1) >> 1).astype(F32).astype(BF16)

    def plane_sums(z):
        row_of = dot(jnp.broadcast_to(row_at[z], (8, 128)).astype(BF16), twice)[0:1].astype(I32) - 1
        data = got_s[pl.ds(z * NX, NX)].reshape(NX * 8, 512)
        parts = []
        for h in range(2):
            hit = (iota((ROWS, 2 * 128), 0) == jnp.where(half == h, row_of, -1)).astype(F32).astype(BF16)
            parts.append(dot(hit, data))
        return parts

    def add_plane(z, first):
        phase("plane")
        for h, part in enumerate(plane_sums(z)):
            lanes = slice(h * 512, (h + 1) * 512)
            sums[:, lanes] = part if first else sums[:, lanes] + part

    for i, side in enumerate(SIDES):
        if i == 1:
            add_plane(mz, True)
        choose_some(1)
        phase("relay")
        for way in range(2):
            ring_copy(side, way).wait_recv()
            relay_copy(side, way).start()
    for i in range(2):
        phase("rows")
        row_copy(i).wait_recv()
        add_plane((down, up)[i], False)
    choose_some(8)
    phase("arrive")
    row_copy(2).wait_recv()
    for side in SIDES:
        for way in range(2):
            relay_copy(side, way).wait_recv()

    phase("sums")
    for h, part in enumerate(plane_sums(across)):
        part = part + sums[:, h * 512 : (h + 1) * 512]
        for k in range(4):
            rows[pl.ds(h * 4 + k, ROWS, stride=TERMS), :] = part[:, k * 128 : (k + 1) * 128]

    phase("binning")
    lane_row = (iota((PANELS, 128), 1) >> 3).astype(F32).astype(BF16)

    @pl.loop(0, ROWS // 16 // UNROLL)
    def _(turn):
        for u in range(UNROLL):
            group = turn * UNROLL + u
            part = rows[pl.ds(pl.multiple_of(group * 128, 128), 128), :].astype(BF16).astype(F32)
            high = bins[pl.ds(group * 16 * NZ + mz, 16, stride=NZ), :] >> 7
            high = [jnp.broadcast_to(high[g : g + 1, :], (TERMS, PANELS)) for g in range(16)]
            zero = jnp.where(jnp.concatenate(high, axis=0) == 0, part, 0.0)
            flats = [flat.T.astype(BF16) for flat in (zero, part - zero)]
            zeros = jnp.zeros((), BF16)
            wide = [
                jnp.concatenate([jnp.where(lane_row == g, flat, zeros) for flat in flats], axis=1)
                for g in range(16)
            ]
            tall = jnp.concatenate([weights[group * 16 + g] for g in range(16)], axis=1)
            value = dot(tall, jnp.concatenate(wide, axis=0))
            low, high = value[0:HALF, 0:128], value[0:HALF, 128:256]
            carried = high[0:8] + value[HALF : HALF + 8, 0:128]
            arrived[group, 0:HALF, :] = low.astype(BF16)
            arrived[group, HALF:NBIN, :] = jnp.concatenate([carried, high[8:]], axis=0).astype(BF16)

    phase("signals")
    core = lax.rem(mx, 2)
    chip_x = (mx // 2) & 3
    sibling = mx + 1 - 2 * core
    near_half = chip_x >> 1

    def tiles_of(c):
        sides = (2, 1 + 2 * c, 3 - 2 * c, 0)
        halves = (1 - c, 1, 0, 1 - c)
        return [((my + side) & 3, (near_half + half) & 1) for side, half in zip(sides, halves)]

    theirs, mine = tiles_of(1 - core), tiles_of(core)

    def times_of(tiles):
        tall = jnp.concatenate([arrived[group] for group in range(16)], axis=1)
        value = dot(tall, jnp.concatenate([chosen[2 * y + half] for y, half in tiles], axis=1))
        return [value[:, i * 256 : (i + 1) * 256].T.reshape(32, 8, NBIN) for i in range(2)]

    def pair_copy(i):
        return pltpu.make_async_remote_copy(
            src_ref=send_q.at[i], dst_ref=got_q.at[i], send_sem=qs_sem.at[i], recv_sem=qr_sem.at[i],
            device_id={"gx": sibling, "gy": mz}, device_id_type=MESH,
        )

    def part_copy(tile, dx, dz, dc):
        y, half = mine[tile]
        x, c, z = ((chip_x + dx) & 1) + 2 * half, (core + dc) & 1, (mz + dz) & 3
        return pltpu.make_async_remote_copy(
            src_ref=send_p.at[tile, ((x & 1) * 2 + c) * NZ + z], dst_ref=got_p.at[mz * 16 + mx // 2],
            send_sem=sp_sem, recv_sem=rp_sem,
            device_id={"gx": y * 8 + x * 2 + c, "gy": z}, device_id_type=MESH,
        )

    for i, value in enumerate(times_of(theirs)):
        send_q[i] = value.astype(BF16)
        pair_copy(i).start()
    for i, value in enumerate(times_of(mine)):
        pair_copy(i).wait_recv()
        value = (value + got_q[i].astype(F32)).astype(BF16)
        for tile in (2 * i, 2 * i + 1):
            send_p[tile] = value[(tile & 1) * 16 : (tile & 1) * 16 + 16]
            for dz in (2, 1, 3, 0):
                for dx in (1, 0):
                    for dc in (1, 0):
                        if tile < 3 or dx or dz or dc:
                            part_copy(tile, dx, dz, dc).start()

    phase("collect")
    keeps = core == 1

    @pl.when(keeps)
    def _():
        got_p[mz * 16 + mx // 2] = send_p[3, ((chip_x & 1) * 2 + core) * NZ + mz]
        wait_bytes(got_p, 63, rp_sem)
        wait_bytes(got_p, 63, sp_sem)

    @pl.when(jnp.logical_not(keeps))
    def _():
        part_copy(3, 0, 0, 0).start()
        wait_bytes(got_p, 64, rp_sem)
        wait_bytes(got_p, 64, sp_sem)

    phase("total")
    for o in range(NZ):
        total = jnp.zeros((8, NBIN), F32)
        for i in range(16):
            total = total + got_p[o * 16 + i].astype(F32)
        out_ref[o] = total
    phase("drain")
    wait_bytes(got_s, NX - 1, ss_sem)
    wait_bytes(got_m, NX - 1, sm_sem)
    if DIRECT:
        wait_bytes(got_s, 16 * len(DIRECT), ds_sem)
    for i in range(2):
        pair_copy(i).wait_send()
    for i in range(3):
        row_copy(i).wait_send()
    for side in SIDES:
        for way in range(2):
            if side not in DIRECT:
                ring_copy(side, way).wait_send()
            relay_copy(side, way).wait_send()
    phase()


def on_device(sources, owners, strip_rows, panel_counts, arrival_bins, arrival_fracs, gain_table):
    any_space = pl.BlockSpec(memory_space=pl.ANY)
    vmem = pl.BlockSpec(memory_space=pltpu.VMEM)
    gains = gain_table.reshape(ROWS * TERMS, NZ, 8, 128).transpose(0, 2, 1, 3)
    gains = gains.reshape(ROWS * TERMS, 8, 2, 2, 128)
    dma = pltpu.SemaphoreType.DMA
    out = pl.pallas_call(
        kernel,
        out_shape=pltpu.VMEM((NZ, 8, NBIN), F32),
        in_specs=[any_space] * 7,
        out_specs=vmem,
        scratch_shapes=[
            pltpu.VMEM((NX, 8, 512), BF16),
            pltpu.VMEM((NX, 1, 128), F32),
            pltpu.VMEM((ND, 8, 512), BF16),
            pltpu.VMEM((NX, 1, 128), F32),
            pltpu.VMEM((ROWS * NZ, PANELS), I32),
            pltpu.VMEM((ROWS * NZ, PANELS), F32),
            pltpu.VMEM((8, ROWS * TERMS, 2, 128), BF16),
            pltpu.VMEM((ROWS, TALL, PANELS), BF16),
            pltpu.VMEM((ROWS * TERMS, PANELS), F32),
            pltpu.VMEM((16, NBIN, 128), BF16),
            pltpu.VMEM((8, ROWS * TERMS, 128), BF16),
            pltpu.VMEM((128, 256), BF16),
            pltpu.VMEM((ROWS, TERMS * PANELS), F32),
            pltpu.VMEM((NZ, 1, 128), F32),
            pltpu.VMEM((2, 32, 8, NBIN), BF16),
            pltpu.VMEM((2, 32, 8, NBIN), BF16),
            pltpu.VMEM((4, 16, 8, NBIN), BF16),
            pltpu.VMEM((64, 8, NBIN), BF16),
            dma((6,)), dma((8,)), dma, dma, dma, dma((4,)), dma, dma,
            dma((2, 4)), dma((2, 4)), dma((2, 4)), dma((2, 4)), dma((3,)), dma((3,)), dma((2,)), dma((2,)), dma,
            pltpu.VMEM((STRIPS * TERMS, PANELS), BF16),
            pltpu.VMEM((1, STRIPS), I32), pltpu.VMEM((1, STRIPS), I32), pltpu.VMEM((1, STRIPS), I32),
        ],
        compiler_params=pltpu.CompilerParams(
            collective_id=0, has_side_effects=True, vmem_limit_bytes=60 * 1024 * 1024
        ),
    )(
        sources.reshape(STRIPS * TERMS, PANELS),
        owners.reshape(1, STRIPS),
        strip_rows.reshape(1, STRIPS),
        panel_counts.reshape(1, STRIPS),
        arrival_bins.reshape(ROWS * NZ, PANELS),
        arrival_fracs.reshape(ROWS * NZ, PANELS),
        gains,
    )
    return out.transpose(1, 0, 2)


def solution(mesh):
    placed = (
        P(("gx", "gy"), None, None),
        P(("gx", "gy"), None),
        P(("gx", "gy")),
        P(("gx", "gy")),
        P("gx", None, None),
        P("gx", None, None),
        P("gx", None, None, None),
    )
    return jax.shard_map(
        on_device,
        mesh=mesh,
        in_specs=placed,
        out_specs=P(("gx", "gy"), None, None),
        check_vma=False,
    )
```

profile of v0, /device:TPU:1, one launch (start us, length us, event | category | flops | bytes accessed | tf_op | source)
XLA Modules:
  0.0 39.1 jit_solution(6687889221519744790)
XLA Ops:
  0.0 38.5 %shard_map.73 = f32[4,8,256]{2,1,0:T(8,128)S(1)} custom-call(bf16[512,128]{1,0:T(8,128)(2,1)} %bitcast.16, s32[1,64]{1,0:T(1,128)} %bitcast.17, s32[1,64]{1,0:T(1,128)} %bitcast.18, s32[1,64]{1,0:T(1,128)} %bitcast.19, s32[1024,128]{1,0:T(8,128)} %bitcast.14, f32[1024,128]{1,0:T(8,128)} %bitcast.15, bf16[2048,8,2,2,128]{4,3,2,1,0:T(2,128)(2,1)} %bitcast.13), custom_call_target="tpu_custom_call" | custom-call | tf_op jit(solution)/shard_map/pallas_call | solution.py:431
  38.5 0.6 %copy.9 = f32[8,4,256]{2,1,0:T(4,128)} copy(f32[8,4,256]{2,0,1:T(8,128)S(1)} %bitcast.12) | data formatting | bytes 65536 | tf_op jit(solution)/shard_map/transpose | solution.py:472
where the time goes:
time: 39.3 us; the launch traced here: 39.1 us
  Pallas kernels  38.5 us (98%)
  local copies, waits for them, and re-layouts  0.63 us (2%)
    pallas_call x1, Pallas kernels, on_device(): pl.pallas_call(kernel, out_shape=pltpu.VMEM((NZ, 8, NBIN), F32), in_specs...  38.5 us

commit v1 on v0

--- a/solution.py
+++ b/solution.py
@@ -22,7 +22,6 @@
 TIMES = 1024
 HALF = NBIN // 2
 TALL = HALF + 16
-UNROLL = 4
 NT = (((1,), (1,)), ((), ()))
 
 
@@ -68,26 +67,6 @@
     def gain_copy(tile):
         return pltpu.make_async_copy(gains_hbm.at[:, tile, mz // 2], gains.at[tile], gain_sem.at[tile])
 
-    barrier = pltpu.get_barrier_semaphore()
-    up, down, across = (lax.rem(mz + i, NZ) for i in (1, 3, 2))
-
-    @pl.loop(1, NX)
-    def _(step):
-        peer = lax.rem(mx + step, NX)
-        pl.semaphore_signal(barrier, inc=1, device_id={"gx": peer, "gy": mz}, device_id_type=MESH)
-
-    pl.semaphore_signal(barrier, inc=1, device_id={"gx": mx, "gy": across}, device_id_type=MESH)
-
-    if not DIRECT:
-        for plane in (up, down):
-            pl.semaphore_signal(barrier, inc=1, device_id={"gx": mx, "gy": plane}, device_id_type=MESH)
-
-    @pl.loop(0, 8 * len(DIRECT))
-    def _(step):
-        peer = (mx // 8 * 8 + step // 8 * 8 + lax.rem(mx + step, 8)) & (NX - 1)
-        for plane in (up, down):
-            pl.semaphore_signal(barrier, inc=1, device_id={"gx": peer, "gy": plane}, device_id_type=MESH)
-
     small = [
         pltpu.make_async_copy(hbm, ref, in_sem.at[2 + i])
         for i, (hbm, ref) in enumerate(
@@ -100,6 +79,26 @@
     fracs_copy = pltpu.make_async_copy(fracs_hbm, fracs, in_sem.at[1])
     bins_copy.start()
     fracs_copy.start()
+
+    barrier = pltpu.get_barrier_semaphore()
+    up, down, across = (lax.rem(mz + i, NZ) for i in (1, 3, 2))
+
+    @pl.loop(1, NX)
+    def _(step):
+        peer = lax.rem(mx + step, NX)
+        pl.semaphore_signal(barrier, inc=1, device_id={"gx": peer, "gy": mz}, device_id_type=MESH)
+
+    pl.semaphore_signal(barrier, inc=1, device_id={"gx": mx, "gy": across}, device_id_type=MESH)
+
+    if not DIRECT:
+        for plane in (up, down):
+            pl.semaphore_signal(barrier, inc=1, device_id={"gx": mx, "gy": plane}, device_id_type=MESH)
+
+    @pl.loop(0, 8 * len(DIRECT))
+    def _(step):
+        peer = (mx // 8 * 8 + step // 8 * 8 + lax.rem(mx + step, 8)) & (NX - 1)
+        for plane in (up, down):
+            pl.semaphore_signal(barrier, inc=1, device_id={"gx": peer, "gy": plane}, device_id_type=MESH)
 
     def weigh(first, last):
         where_b = iota((TALL, PANELS), 0).astype(F32).astype(BF16)
@@ -141,9 +140,10 @@
     live = iota((STRIPS * TERMS, PANELS), 1).astype(F32) < count
     masked = jnp.where(live, src_ref[...].astype(F32), 0.0).astype(BF16)
     term = iota((1, STRIPS * TERMS), 1) & 7
+    slot_rows = iota((ND * 2, STRIPS * TERMS), 0).astype(F32).astype(BF16)
     for kk in range(4):
-        dest = jnp.where((term & 3) == kk, 2 * slot_c + (term >> 2), -1)
-        placing = (iota((ND * 2, STRIPS * TERMS), 0) == dest).astype(F32).astype(BF16)
+        dest = jnp.where((term & 3) == kk, 2 * slot_c + (term >> 2), -1).astype(F32).astype(BF16)
+        placing = jnp.where(slot_rows == dest, jnp.ones((), BF16), jnp.zeros((), BF16))
         placed = dot(placing, masked)
         send_s[:, :, kk * 128 : (kk + 1) * 128] = placed.reshape(NX, 8, 128).astype(BF16)
 
@@ -273,18 +273,20 @@
     half = iota((1, 2 * ND), 1) & 1
     twice = (iota((128, 2 * 128), 0) == iota((128, 2 * 128), 1) >> 1).astype(F32).astype(BF16)
 
-    def plane_sums(z):
-        row_of = dot(jnp.broadcast_to(row_at[z], (8, 128)).astype(BF16), twice)[0:1].astype(I32) - 1
+    row_ids = iota((ROWS, 2 * 128), 0).astype(F32).astype(BF16)
+
+    def plane_hits(z):
+        row_of = dot(jnp.broadcast_to(row_at[z], (8, 128)).astype(BF16), twice)[0:1] - 1.0
+        hits = [jnp.where(half == h, row_of, -1.0).astype(BF16) for h in range(2)]
+        return [jnp.where(row_ids == hit, jnp.ones((), BF16), jnp.zeros((), BF16)) for hit in hits]
+
+    def plane_sums(z, hits):
         data = got_s[pl.ds(z * NX, NX)].reshape(NX * 8, 512)
-        parts = []
-        for h in range(2):
-            hit = (iota((ROWS, 2 * 128), 0) == jnp.where(half == h, row_of, -1)).astype(F32).astype(BF16)
-            parts.append(dot(hit, data))
-        return parts
+        return [dot(hit, data) for hit in hits]
 
     def add_plane(z, first):
         phase("plane")
-        for h, part in enumerate(plane_sums(z)):
+        for h, part in enumerate(plane_sums(z, plane_hits(z))):
             lanes = slice(h * 512, (h + 1) * 512)
             sums[:, lanes] = part if first else sums[:, lanes] + part
 
@@ -303,12 +305,13 @@
     choose_some(8)
     phase("arrive")
     row_copy(2).wait_recv()
+    last_hits = plane_hits(across)
     for side in SIDES:
         for way in range(2):
             relay_copy(side, way).wait_recv()
 
     phase("sums")
-    for h, part in enumerate(plane_sums(across)):
+    for h, part in enumerate(plane_sums(across, last_hits)):
         part = part + sums[:, h * 512 : (h + 1) * 512]
         for k in range(4):
             rows[pl.ds(h * 4 + k, ROWS, stride=TERMS), :] = part[:, k * 128 : (k + 1) * 128]
@@ -316,26 +319,23 @@
     phase("binning")
     lane_row = (iota((PANELS, 128), 1) >> 3).astype(F32).astype(BF16)
 
-    @pl.loop(0, ROWS // 16 // UNROLL)
-    def _(turn):
-        for u in range(UNROLL):
-            group = turn * UNROLL + u
-            part = rows[pl.ds(pl.multiple_of(group * 128, 128), 128), :].astype(BF16).astype(F32)
-            high = bins[pl.ds(group * 16 * NZ + mz, 16, stride=NZ), :] >> 7
-            high = [jnp.broadcast_to(high[g : g + 1, :], (TERMS, PANELS)) for g in range(16)]
-            zero = jnp.where(jnp.concatenate(high, axis=0) == 0, part, 0.0)
-            flats = [flat.T.astype(BF16) for flat in (zero, part - zero)]
-            zeros = jnp.zeros((), BF16)
-            wide = [
-                jnp.concatenate([jnp.where(lane_row == g, flat, zeros) for flat in flats], axis=1)
-                for g in range(16)
-            ]
-            tall = jnp.concatenate([weights[group * 16 + g] for g in range(16)], axis=1)
-            value = dot(tall, jnp.concatenate(wide, axis=0))
-            low, high = value[0:HALF, 0:128], value[0:HALF, 128:256]
-            carried = high[0:8] + value[HALF : HALF + 8, 0:128]
-            arrived[group, 0:HALF, :] = low.astype(BF16)
-            arrived[group, HALF:NBIN, :] = jnp.concatenate([carried, high[8:]], axis=0).astype(BF16)
+    for batch in range(ROWS // 16):
+        part = rows[batch * 128 : (batch + 1) * 128, :].astype(BF16).astype(F32)
+        high = bins[pl.ds(batch * 16 * NZ + mz, 16, stride=NZ), :] >> 7
+        high = [jnp.broadcast_to(high[g : g + 1, :], (TERMS, PANELS)) for g in range(16)]
+        zero = jnp.where(jnp.concatenate(high, axis=0) == 0, part, 0.0)
+        flats = [flat.T.astype(BF16) for flat in (zero, part - zero)]
+        zeros = jnp.zeros((), BF16)
+        wide = [
+            jnp.concatenate([jnp.where(lane_row == g, flat, zeros) for flat in flats], axis=1)
+            for g in range(16)
+        ]
+        tall = jnp.concatenate([weights[batch * 16 + g] for g in range(16)], axis=1)
+        value = dot(tall, jnp.concatenate(wide, axis=0))
+        low, high = value[0:HALF, 0:128], value[0:HALF, 128:256]
+        carried = high[0:8] + value[HALF : HALF + 8, 0:128]
+        arrived[batch, 0:HALF, :] = low.astype(BF16)
+        arrived[batch, HALF:NBIN, :] = jnp.concatenate([carried, high[8:]], axis=0).astype(BF16)
 
     phase("signals")
     core = lax.rem(mx, 2)

time: 39.3 us -> 38.3 us (0.975)
  Pallas kernels: 38.5 us -> 37.5 us
    pallas_call x1, Pallas kernels: 38.5 us -> 37.5 us  [on_device(): pl.pallas_call(kernel, out_shape=pltpu.VMEM((NZ, 8, NBIN), F32), in_specs...]
where the time goes in v1:
time: 38.3 us; the launch traced here: 38.2 us
  Pallas kernels  37.5 us (98%)
  local copies, waits for them, and re-layouts  0.63 us (2%)
    pallas_call x1, Pallas kernels, on_device(): pl.pallas_call(kernel, out_shape=pltpu.VMEM((NZ, 8, NBIN), F32), in_specs...  37.5 us

profile of v1, /device:TPU:1, one launch (start us, length us, event | category | flops | bytes accessed | tf_op | source)
XLA Modules:
  0.0 38.2 jit_solution(15541875524766025038)
XLA Ops:
  0.0 37.5 %shard_map.73 = f32[4,8,256]{2,1,0:T(8,128)S(1)} custom-call(bf16[512,128]{1,0:T(8,128)(2,1)} %bitcast.16, s32[1,64]{1,0:T(1,128)} %bitcast.17, s32[1,64]{1,0:T(1,128)} %bitcast.18, s32[1,64]{1,0:T(1,128)} %bitcast.19, s32[1024,128]{1,0:T(8,128)} %bitcast.14, f32[1024,128]{1,0:T(8,128)} %bitcast.15, bf16[2048,8,2,2,128]{4,3,2,1,0:T(2,128)(2,1)} %bitcast.13), custom_call_target="tpu_custom_call" | custom-call | tf_op jit(solution)/shard_map/pallas_call | solution.py:431
  37.5 0.6 %copy.9 = f32[8,4,256]{2,1,0:T(4,128)} copy(f32[8,4,256]{2,0,1:T(8,128)S(1)} %bitcast.12) | data formatting | bytes 65536 | tf_op jit(solution)/shard_map/transpose | solution.py:472

commit v2 on v1

--- a/solution.py
+++ b/solution.py
@@ -38,7 +38,6 @@
 
 
 SIDES = (0, 1, 3, 2)
-DIRECT = ()
 
 
 def wait_bytes(ref, blocks, sem):
@@ -50,7 +49,7 @@
     src_hbm, own_hbm, row_hbm, cnt_hbm, bins_hbm, fracs_hbm, gains_hbm, out_ref,
     send_s, send_m, got_s, got_m, bins, fracs, gains, weights, rows, arrived,
     chosen, select, sums, row_at, send_q, got_q, send_p, got_p, in_sem, gain_sem, ss_sem, sm_sem, sp_sem, rs_sem, rm_sem, rp_sem,
-    zs_sem, zr_sem, za_sem, zb_sem, ms_sem, mr_sem, qs_sem, qr_sem, ds_sem,
+    zr_sem, zb_sem, ms_sem, mr_sem, qs_sem, qr_sem,
     src_ref, own_ref, row_ref, cnt_ref,
 ):
     mx = lax.axis_index("gx")
@@ -65,7 +64,7 @@
             scopes[-1].__enter__()
 
     def gain_copy(tile):
-        return pltpu.make_async_copy(gains_hbm.at[:, tile, mz // 2], gains.at[tile], gain_sem.at[tile])
+        return pltpu.make_async_copy(gains_hbm.at[:, tile, mz // 2], gains.at[tile], gain_sem)
 
     small = [
         pltpu.make_async_copy(hbm, ref, in_sem.at[2 + i])
@@ -90,15 +89,8 @@
 
     pl.semaphore_signal(barrier, inc=1, device_id={"gx": mx, "gy": across}, device_id_type=MESH)
 
-    if not DIRECT:
-        for plane in (up, down):
-            pl.semaphore_signal(barrier, inc=1, device_id={"gx": mx, "gy": plane}, device_id_type=MESH)
-
-    @pl.loop(0, 8 * len(DIRECT))
-    def _(step):
-        peer = (mx // 8 * 8 + step // 8 * 8 + lax.rem(mx + step, 8)) & (NX - 1)
-        for plane in (up, down):
-            pl.semaphore_signal(barrier, inc=1, device_id={"gx": peer, "gy": plane}, device_id_type=MESH)
+    for plane in (up, down):
+        pl.semaphore_signal(barrier, inc=1, device_id={"gx": mx, "gy": plane}, device_id_type=MESH)
 
     def weigh(first, last):
         where_b = iota((TALL, PANELS), 0).astype(F32).astype(BF16)
@@ -148,7 +140,7 @@
         send_s[:, :, kk * 128 : (kk + 1) * 128] = placed.reshape(NX, 8, 128).astype(BF16)
 
     phase("barrier")
-    pl.semaphore_wait(barrier, NX + (16 * len(DIRECT) or 2))
+    pl.semaphore_wait(barrier, NX - 1 + NZ - 1)
 
     my = mx // 8
 
@@ -162,13 +154,6 @@
         return pltpu.make_async_remote_copy(
             src_ref=send_m.at[j], dst_ref=got_m.at[mx], send_sem=sm_sem, recv_sem=rm_sem,
             device_id={"gx": j, "gy": mz}, device_id_type=MESH,
-        )
-
-    def direct_copy(j, side, way):
-        return pltpu.make_async_remote_copy(
-            src_ref=send_s.at[j], dst_ref=got_s.at[mz * NX + mx], send_sem=ds_sem,
-            recv_sem=zr_sem.at[way, side], device_id={"gx": j, "gy": (up, down)[way]},
-            device_id_type=MESH,
         )
 
     phase("send")
@@ -181,12 +166,6 @@
     def _(step):
         meta_copy(lax.rem(mx + step, NX)).start()
 
-    for side in DIRECT:
-        for i in range(8):
-            j = lax.rem(my + NZ - side, 4) * 8 + lax.rem(mx + i, 8)
-            for way in range(2):
-                direct_copy(j, side, way).start()
-
     for tile in range(8):
         gain_copy(tile).start()
     got_s[mz * NX + mx] = send_s[mx]
@@ -201,7 +180,7 @@
     def ring_copy(side, way):
         block = group(mz, side)
         return pltpu.make_async_remote_copy(
-            src_ref=block, dst_ref=block, send_sem=zs_sem.at[way, side],
+            src_ref=block, dst_ref=block, send_sem=ss_sem,
             recv_sem=zr_sem.at[way, side], device_id={"gx": mx, "gy": (up, down)[way]},
             device_id_type=MESH,
         )
@@ -209,8 +188,8 @@
     def relay_copy(side, way):
         block = group((down, up)[way], side, way)
         return pltpu.make_async_remote_copy(
-            src_ref=block, dst_ref=block, send_sem=za_sem.at[way, side],
-            recv_sem=zb_sem.at[way, side], device_id={"gx": mx, "gy": (up, down)[way]},
+            src_ref=block, dst_ref=block, send_sem=ss_sem,
+            recv_sem=zb_sem, device_id={"gx": mx, "gy": (up, down)[way]},
             device_id_type=MESH,
         )
 
@@ -250,11 +229,10 @@
     for i, side in enumerate(SIDES):
         phase("near")
         wait_bytes(got_s, 8 if side else 7, rs_sem.at[side])
-        for way in range(0 if side in DIRECT else 2):
+        for way in range(2):
             ring_copy(side, way).start()
         if i == 0:
-            for tile in range(8):
-                gain_copy(tile).wait()
+            pltpu.make_async_copy(gains, gains, gain_sem).wait()
         choose_some(1)
     phase("meta")
     wait_bytes(got_m, NX - 1, rm_sem)
@@ -263,7 +241,7 @@
     def row_copy(i):
         peer = (up, down, across)[i]
         return pltpu.make_async_remote_copy(
-            src_ref=row_at.at[mz], dst_ref=row_at.at[mz], send_sem=ms_sem.at[i],
+            src_ref=row_at.at[mz], dst_ref=row_at.at[mz], send_sem=ms_sem,
             recv_sem=mr_sem.at[i], device_id={"gx": mx, "gy": peer}, device_id_type=MESH,
         )
 
@@ -306,9 +284,7 @@
     phase("arrive")
     row_copy(2).wait_recv()
     last_hits = plane_hits(across)
-    for side in SIDES:
-        for way in range(2):
-            relay_copy(side, way).wait_recv()
+    wait_bytes(got_s, 32, zb_sem)
 
     phase("sums")
     for h, part in enumerate(plane_sums(across, last_hits)):
@@ -357,7 +333,7 @@
 
     def pair_copy(i):
         return pltpu.make_async_remote_copy(
-            src_ref=send_q.at[i], dst_ref=got_q.at[i], send_sem=qs_sem.at[i], recv_sem=qr_sem.at[i],
+            src_ref=send_q.at[i], dst_ref=got_q.at[i], send_sem=qs_sem, recv_sem=qr_sem.at[i],
             device_id={"gx": sibling, "gy": mz}, device_id_type=MESH,
         )
 
@@ -406,19 +382,10 @@
             total = total + got_p[o * 16 + i].astype(F32)
         out_ref[o] = total
     phase("drain")
-    wait_bytes(got_s, NX - 1, ss_sem)
+    wait_bytes(got_s, NX - 1 + 64 + 32, ss_sem)
     wait_bytes(got_m, NX - 1, sm_sem)
-    if DIRECT:
-        wait_bytes(got_s, 16 * len(DIRECT), ds_sem)
-    for i in range(2):
-        pair_copy(i).wait_send()
-    for i in range(3):
-        row_copy(i).wait_send()
-    for side in SIDES:
-        for way in range(2):
-            if side not in DIRECT:
-                ring_copy(side, way).wait_send()
-            relay_copy(side, way).wait_send()
+    wait_bytes(row_at, 3, ms_sem)
+    wait_bytes(send_q, 2, qs_sem)
     phase()
 
 
@@ -452,8 +419,8 @@
             pltpu.VMEM((2, 32, 8, NBIN), BF16),
             pltpu.VMEM((4, 16, 8, NBIN), BF16),
             pltpu.VMEM((64, 8, NBIN), BF16),
-            dma((6,)), dma((8,)), dma, dma, dma, dma((4,)), dma, dma,
-            dma((2, 4)), dma((2, 4)), dma((2, 4)), dma((2, 4)), dma((3,)), dma((3,)), dma((2,)), dma((2,)), dma,
+            dma((6,)), dma, dma, dma, dma, dma((4,)), dma, dma,
+            dma((2, 4)), dma, dma, dma((3,)), dma, dma((2,)),
             pltpu.VMEM((STRIPS * TERMS, PANELS), BF16),
             pltpu.VMEM((1, STRIPS), I32), pltpu.VMEM((1, STRIPS), I32), pltpu.VMEM((1, STRIPS), I32),
         ],

time: 38.3 us -> 38 us (level)
  no operation moved by 1% of the time
where the time goes in v2:
time: 38 us; the launch traced here: 37.8 us
  Pallas kernels  37.2 us (98%)
  local copies, waits for them, and re-layouts  0.63 us (2%)
    pallas_call x1, Pallas kernels, on_device(): pl.pallas_call(kernel, out_shape=pltpu.VMEM((NZ, 8, NBIN), F32), in_specs...  37.2 us

profile of v2, /device:TPU:1, one launch (start us, length us, event | category | flops | bytes accessed | tf_op | source)
XLA Modules:
  0.0 37.8 jit_solution(10074317200530986832)
XLA Ops:
  0.0 37.2 %shard_map.73 = f32[4,8,256]{2,1,0:T(8,128)S(1)} custom-call(bf16[512,128]{1,0:T(8,128)(2,1)} %bitcast.16, s32[1,64]{1,0:T(1,128)} %bitcast.17, s32[1,64]{1,0:T(1,128)} %bitcast.18, s32[1,64]{1,0:T(1,128)} %bitcast.19, s32[1024,128]{1,0:T(8,128)} %bitcast.14, f32[1024,128]{1,0:T(8,128)} %bitcast.15, bf16[2048,8,2,2,128]{4,3,2,1,0:T(2,128)(2,1)} %bitcast.13), custom_call_target="tpu_custom_call" | custom-call | tf_op jit(solution)/shard_map/pallas_call | solution.py:398
  37.2 0.6 %copy.9 = f32[8,4,256]{2,1,0:T(4,128)} copy(f32[8,4,256]{2,0,1:T(8,128)S(1)} %bitcast.12) | data formatting | bytes 65536 | tf_op jit(solution)/shard_map/transpose | solution.py:439
